TPU v7x, 32 devices: a whole 2x2x4 slice. The times are simulated.
32 devices in a mesh: node: 4 (over y, x), row: 8 (over z, core).
Axes of the slice: x: 2, y: 2, z: 4, core: 2. Of those that a mesh axis runs over, the one named last changes fastest.
Arguments:
- inputs: float32 [16, 32, 128, 128], P(None, 'row'), may hold values from -8 to 8
- diagonal: float32 [32, 128, 128], P('row'), may hold values from 0.05 to 1
- observations: float32 [16, 32, 128, 128], P(None, 'row'), may hold values from -0.0078125 to 0.0078125
- frequencies: float32 [4], replicated, may hold values from 0.2 to 3
- weights: float32 [4], replicated, may hold values from 0.5 to 2
- counts: int32 [4], replicated, may hold values from 3 to 6, as said below
- assignment: int32 [4], replicated, may hold values from 0 to 3, each once
Outputs:
- probe_response: float32 [16, 32, 128, 128], P(None, 'row')
- group_gram: float32 [4, 16, 16], P('node')
Inputs may be any that keep to these rules, and one draw needn't show every extreme that they name: `counts`: some node has 6 sweeps and some node 3 in every draw. `assignment`: each node 0 to 3 appears once.
All inputs are finite; a program needn't handle non-finite values.
Results may differ from a plain program's by a relative error of at most 0.0003.
Values sent between devices are 32-bit elements; how exact they have to be, the bound alone decides.
A program may use at most 192 MiB of HBM per device.

v0:
```python
import jax
import jax.numpy as jnp
from jax import lax
from jax.sharding import PartitionSpec as P

NODE_DEV = 1
ITERS = 6


def with_halo(block, sides, width):
    for axis, dim in sides:
        count = lax.axis_size(axis)
        forward = [(i, i + 1) for i in range(count - 1)]
        backward = [(target, source) for source, target in forward]
        low = lax.ppermute(
            lax.slice_in_dim(block, block.shape[dim] - width, None, axis=dim), axis, forward
        )
        high = lax.ppermute(lax.slice_in_dim(block, 0, width, axis=dim), axis, backward)
        block = jnp.concatenate([low, block, high], axis=dim)
    return block


def relax_step(fields, beyond, source, diagonal, shift_col, active):
    padded = jnp.pad(fields, ((0, 0), (0, 0), (0, 0), (0, 0), (1, 1), (1, 1)))
    beside = beyond[:, :, :, 2:] + beyond[:, :, :, :-2]
    beside = beside + padded[:, :, :, :, 2:, 1:-1] + padded[:, :, :, :, :-2, 1:-1]
    beside = beside + padded[:, :, :, :, 1:-1, 2:] + padded[:, :, :, :, 1:-1, :-2]
    diag_full = 6.0 + diagonal
    applied = diag_full * fields - beside
    resid_real = source - applied[:, 0] + shift_col * fields[:, 1]
    resid_imag = -applied[:, 1] - shift_col * fields[:, 0]
    denominator = diag_full * diag_full + shift_col * shift_col
    step_real = (diag_full * resid_real + shift_col * resid_imag) / denominator
    step_imag = (diag_full * resid_imag - shift_col * resid_real) / denominator
    return fields + active * jnp.stack([step_real, step_imag], 1)


def local(inputs, diagonal, observations, frequencies, weights, counts, assignment):
    group_id = lax.axis_index("node")
    my_nodes = lax.dynamic_slice_in_dim(assignment, group_id * NODE_DEV, NODE_DEV)
    quad_count = frequencies.shape[0]
    lookup = my_nodes[:, None] == jnp.arange(quad_count, dtype=jnp.int32)[None, :]
    my_freqs = jnp.sum(jnp.where(lookup, frequencies[None, :], 0.0), 1)
    my_weights = jnp.sum(jnp.where(lookup, weights[None, :], 0.0), 1)
    my_counts = jnp.sum(jnp.where(lookup, counts[None, :], 0), 1)
    planes = inputs.shape[1]
    shift_col = my_freqs.reshape(NODE_DEV, 1, 1, 1, 1)
    start_fields = jnp.zeros((NODE_DEV, 2) + inputs.shape, jnp.float32)

    def sweep_once(sweep, fields):
        beyond = with_halo(fields, (("row", 3),), 1)
        active = (sweep < my_counts).astype(jnp.float32).reshape(NODE_DEV, 1, 1, 1, 1, 1)
        return relax_step(fields, beyond, inputs, diagonal, shift_col, active)

    fields = lax.fori_loop(0, ITERS, sweep_once, start_fields)
    local_cells = planes * inputs.shape[2] * inputs.shape[3]
    flat_fields = fields.reshape(NODE_DEV, 2, inputs.shape[0], local_cells)
    flat_probe = observations.reshape(observations.shape[0], local_cells)
    projected = jnp.einsum(
        "naic,pc->naip", flat_fields, flat_probe, precision=lax.Precision.HIGHEST
    )
    gram_part = jnp.einsum(
        "naic,najc->nij", flat_fields, flat_fields, precision=lax.Precision.HIGHEST
    )
    projected, gram_part = lax.psum((projected, gram_part), "row")
    total_cells = local_cells * lax.axis_size("row")
    group_gram = (
        jnp.einsum("n,nij->ij", my_weights, gram_part, precision=lax.Precision.HIGHEST)
        / total_cells
    )
    weighted = projected * my_weights.reshape(NODE_DEV, 1, 1, 1)
    share = jnp.einsum("naip,naic->pc", weighted, flat_fields, precision=lax.Precision.HIGHEST)
    summed = lax.psum(share, "node")
    probe_response = (summed / quad_count).reshape(observations.shape)
    return (probe_response, group_gram[None])


def solution(mesh):
    placed = (
        P(None, "row", None, None),
        P("row", None, None),
        P(None, "row", None, None),
        P(),
        P(),
        P(),
        P(),
    )
    return jax.shard_map(
        local,
        mesh=mesh,
        in_specs=placed,
        out_specs=(P(None, "row", None, None), P("node", None, None)),
        check_vma=False,
    )
```

profile of v0, /device:TPU:0, one launch (start us, length us, event | category | flops | bytes accessed | tf_op | source)
XLA Modules:
  0.0 677.6 jit_solution(16696439240070895874)
XLA Ops:
  13.5 447.5 %while.16 = (s32[]{:T(128)}, f32[1,2,16,4,128,128]{5,4,3,2,1,0:T(8,128)}, s32[1]{0:T(128)}, f32[4,128,128]{2,1,0:T(8,128)}, f32[16,4,128,128]{3,2,1,0:T(8,128)},...) while((s32[]{:T(128)}, ...), condition=%wide.region_3.4_spmd.clone, body=%wide.region_2.3_spmd.clone.sunk | while | flops 44236800 | bytes 237502864 | solution.py:55
  19.3 3.7 collective-permute-start
  25.8 4.2 collective-permute-done.1
  30.0 24.3 %fusion.25 = f32[1,2,16,4,128,128]{5,4,3,2,1,0:T(8,128)S(1)} fusion(f32[1,2,16,4,128,128]{5,4,3,2,1,0:T(8,128)} %copy-done, f32[1,2,16,1,128,128]{5,4,3,2,1,0:T(8,128)} %collective-permute-done, f32[1,2,16,1,128,128]{5,4,3,2,1,0:T(8,128)} %collective-permute-done.1, f32[4,128,128]{2,1,0:T(8,128)} %get-tuple-element.259), kind=kLoop, calls=%fused_computation.8.clone.1 | loop fusion | flops 18874368 | bytes 21233664 | tf_op jit(solution)/shard_map/while/body/eval_jaxpr/sub | solution.py:29
  54.3 7.1 %add_divide_fusion.2 = (f32[1,1,16,4,128,128]{5,4,3,2,1,0:T(8,128)}, f32[1,1,16,4,128,128]{5,4,3,2,1,0:T(8,128)}) fusion(f32[4,128,128]{2,1,0:T(8,128)} %get-tuple-element.258, f32[]{:T(128)} %bitcast.45, f32[4,128,128]{2,1,0:T(8,128)} %get-tuple-element.259, f32[1,2,16,4,128,128]{5,4,3,2,1,0:T(8,128)S(1)} %bitcast.49, ...), kind=kLoop, calls=%fused_computation.22.clone.1 | loop fusion | flops 14680064 | bytes 29884420 | tf_op jit(solution)/shard_map/while/body/eval_jaxpr/div | solution.py:33
  61.5 4.7 fusion.26
  66.2 3.2 copy-done.1
  69.4 4.2 broadcast_select_fusion.2
  78.6 25.0 %collective-permute-start = (f32[1,2,16,1,128,128]{5,4,3,2,1,0:T(8,128)}, f32[1,2,16,1,128,128]{5,4,3,2,1,0:T(8,128)}, u32[]{:S(2)}, u32[]{:S(2)}) collective-permute-start(f32[1,2,16,1,128,128]{5,4,3,2,1,0:T(8,128)} %get-tuple-element.260), channel_id=1, source_target_pairs={{0,1},{1,2},{2,3},{3,4},{4,5},{5,6},{6,7},{8,9},{9,10},{10,11},{11... | collective-permute-start | bytes 6291464 | tf_op jit(solution)/shard_map/while/body/eval_jaxpr/ppermute | solution.py:15
  106.4 3.3 collective-permute-done.1
  109.8 24.3 %fusion.25 = f32[1,2,16,4,128,128]{5,4,3,2,1,0:T(8,128)S(1)} fusion(f32[1,2,16,4,128,128]{5,4,3,2,1,0:T(8,128)} %copy-done, f32[1,2,16,1,128,128]{5,4,3,2,1,0:T(8,128)} %collective-permute-done, f32[1,2,16,1,128,128]{5,4,3,2,1,0:T(8,128)} %collective-permute-done.1, f32[4,128,128]{2,1,0:T(8,128)} %get-tuple-element.259), kind=kLoop, calls=%fused_computation.8.clone.1 | loop fusion | flops 18874368 | bytes 21233664 | tf_op jit(solution)/shard_map/while/body/eval_jaxpr/sub | solution.py:29
  134.1 7.1 %add_divide_fusion.2 = (f32[1,1,16,4,128,128]{5,4,3,2,1,0:T(8,128)}, f32[1,1,16,4,128,128]{5,4,3,2,1,0:T(8,128)}) fusion(f32[4,128,128]{2,1,0:T(8,128)} %get-tuple-element.258, f32[]{:T(128)} %bitcast.45, f32[4,128,128]{2,1,0:T(8,128)} %get-tuple-element.259, f32[1,2,16,4,128,128]{5,4,3,2,1,0:T(8,128)S(1)} %bitcast.49, ...), kind=kLoop, calls=%fused_computation.22.clone.1 | loop fusion | flops 14680064 | bytes 29884420 | tf_op jit(solution)/shard_map/while/body/eval_jaxpr/div | solution.py:33
  141.2 4.7 fusion.26
  145.9 3.2 copy-done.1
  149.2 4.2 broadcast_select_fusion.2
  158.3 23.2 %collective-permute-start = (f32[1,2,16,1,128,128]{5,4,3,2,1,0:T(8,128)}, f32[1,2,16,1,128,128]{5,4,3,2,1,0:T(8,128)}, u32[]{:S(2)}, u32[]{:S(2)}) collective-permute-start(f32[1,2,16,1,128,128]{5,4,3,2,1,0:T(8,128)} %get-tuple-element.260), channel_id=1, source_target_pairs={{0,1},{1,2},{2,3},{3,4},{4,5},{5,6},{6,7},{8,9},{9,10},{10,11},{11... | collective-permute-start | bytes 6291464 | tf_op jit(solution)/shard_map/while/body/eval_jaxpr/ppermute | solution.py:15
  184.4 3.3 collective-permute-done.1
  187.7 24.3 %fusion.25 = f32[1,2,16,4,128,128]{5,4,3,2,1,0:T(8,128)S(1)} fusion(f32[1,2,16,4,128,128]{5,4,3,2,1,0:T(8,128)} %copy-done, f32[1,2,16,1,128,128]{5,4,3,2,1,0:T(8,128)} %collective-permute-done, f32[1,2,16,1,128,128]{5,4,3,2,1,0:T(8,128)} %collective-permute-done.1, f32[4,128,128]{2,1,0:T(8,128)} %get-tuple-element.259), kind=kLoop, calls=%fused_computation.8.clone.1 | loop fusion | flops 18874368 | bytes 21233664 | tf_op jit(solution)/shard_map/while/body/eval_jaxpr/sub | solution.py:29
  212.0 7.1 %add_divide_fusion.2 = (f32[1,1,16,4,128,128]{5,4,3,2,1,0:T(8,128)}, f32[1,1,16,4,128,128]{5,4,3,2,1,0:T(8,128)}) fusion(f32[4,128,128]{2,1,0:T(8,128)} %get-tuple-element.258, f32[]{:T(128)} %bitcast.45, f32[4,128,128]{2,1,0:T(8,128)} %get-tuple-element.259, f32[1,2,16,4,128,128]{5,4,3,2,1,0:T(8,128)S(1)} %bitcast.49, ...), kind=kLoop, calls=%fused_computation.22.clone.1 | loop fusion | flops 14680064 | bytes 29884420 | tf_op jit(solution)/shard_map/while/body/eval_jaxpr/div | solution.py:33
  219.2 4.7 fusion.26
  223.9 3.2 copy-done.1
  227.1 4.2 broadcast_select_fusion.2
  236.3 23.2 %collective-permute-start = (f32[1,2,16,1,128,128]{5,4,3,2,1,0:T(8,128)}, f32[1,2,16,1,128,128]{5,4,3,2,1,0:T(8,128)}, u32[]{:S(2)}, u32[]{:S(2)}) collective-permute-start(f32[1,2,16,1,128,128]{5,4,3,2,1,0:T(8,128)} %get-tuple-element.260), channel_id=1, source_target_pairs={{0,1},{1,2},{2,3},{3,4},{4,5},{5,6},{6,7},{8,9},{9,10},{10,11},{11... | collective-permute-start | bytes 6291464 | tf_op jit(solution)/shard_map/while/body/eval_jaxpr/ppermute | solution.py:15
  262.3 3.3 collective-permute-done.1
  265.7 24.3 %fusion.25 = f32[1,2,16,4,128,128]{5,4,3,2,1,0:T(8,128)S(1)} fusion(f32[1,2,16,4,128,128]{5,4,3,2,1,0:T(8,128)} %copy-done, f32[1,2,16,1,128,128]{5,4,3,2,1,0:T(8,128)} %collective-permute-done, f32[1,2,16,1,128,128]{5,4,3,2,1,0:T(8,128)} %collective-permute-done.1, f32[4,128,128]{2,1,0:T(8,128)} %get-tuple-element.259), kind=kLoop, calls=%fused_computation.8.clone.1 | loop fusion | flops 18874368 | bytes 21233664 | tf_op jit(solution)/shard_map/while/body/eval_jaxpr/sub | solution.py:29
  290.0 7.1 %add_divide_fusion.2 = (f32[1,1,16,4,128,128]{5,4,3,2,1,0:T(8,128)}, f32[1,1,16,4,128,128]{5,4,3,2,1,0:T(8,128)}) fusion(f32[4,128,128]{2,1,0:T(8,128)} %get-tuple-element.258, f32[]{:T(128)} %bitcast.45, f32[4,128,128]{2,1,0:T(8,128)} %get-tuple-element.259, f32[1,2,16,4,128,128]{5,4,3,2,1,0:T(8,128)S(1)} %bitcast.49, ...), kind=kLoop, calls=%fused_computation.22.clone.1 | loop fusion | flops 14680064 | bytes 29884420 | tf_op jit(solution)/shard_map/while/body/eval_jaxpr/div | solution.py:33
  297.1 4.7 fusion.26
  301.8 3.2 copy-done.1
  305.1 4.2 broadcast_select_fusion.2
  314.2 23.2 %collective-permute-start = (f32[1,2,16,1,128,128]{5,4,3,2,1,0:T(8,128)}, f32[1,2,16,1,128,128]{5,4,3,2,1,0:T(8,128)}, u32[]{:S(2)}, u32[]{:S(2)}) collective-permute-start(f32[1,2,16,1,128,128]{5,4,3,2,1,0:T(8,128)} %get-tuple-element.260), channel_id=1, source_target_pairs={{0,1},{1,2},{2,3},{3,4},{4,5},{5,6},{6,7},{8,9},{9,10},{10,11},{11... | collective-permute-start | bytes 6291464 | tf_op jit(solution)/shard_map/while/body/eval_jaxpr/ppermute | solution.py:15
  340.3 3.3 collective-permute-done.1
  343.6 24.3 %fusion.25 = f32[1,2,16,4,128,128]{5,4,3,2,1,0:T(8,128)S(1)} fusion(f32[1,2,16,4,128,128]{5,4,3,2,1,0:T(8,128)} %copy-done, f32[1,2,16,1,128,128]{5,4,3,2,1,0:T(8,128)} %collective-permute-done, f32[1,2,16,1,128,128]{5,4,3,2,1,0:T(8,128)} %collective-permute-done.1, f32[4,128,128]{2,1,0:T(8,128)} %get-tuple-element.259), kind=kLoop, calls=%fused_computation.8.clone.1 | loop fusion | flops 18874368 | bytes 21233664 | tf_op jit(solution)/shard_map/while/body/eval_jaxpr/sub | solution.py:29
  367.9 7.1 %add_divide_fusion.2 = (f32[1,1,16,4,128,128]{5,4,3,2,1,0:T(8,128)}, f32[1,1,16,4,128,128]{5,4,3,2,1,0:T(8,128)}) fusion(f32[4,128,128]{2,1,0:T(8,128)} %get-tuple-element.258, f32[]{:T(128)} %bitcast.45, f32[4,128,128]{2,1,0:T(8,128)} %get-tuple-element.259, f32[1,2,16,4,128,128]{5,4,3,2,1,0:T(8,128)S(1)} %bitcast.49, ...), kind=kLoop, calls=%fused_computation.22.clone.1 | loop fusion | flops 14680064 | bytes 29884420 | tf_op jit(solution)/shard_map/while/body/eval_jaxpr/div | solution.py:33
  375.1 4.7 fusion.26
  379.8 3.2 copy-done.1
  383.0 4.2 broadcast_select_fusion.2
  392.2 23.2 %collective-permute-start = (f32[1,2,16,1,128,128]{5,4,3,2,1,0:T(8,128)}, f32[1,2,16,1,128,128]{5,4,3,2,1,0:T(8,128)}, u32[]{:S(2)}, u32[]{:S(2)}) collective-permute-start(f32[1,2,16,1,128,128]{5,4,3,2,1,0:T(8,128)} %get-tuple-element.260), channel_id=1, source_target_pairs={{0,1},{1,2},{2,3},{3,4},{4,5},{5,6},{6,7},{8,9},{9,10},{10,11},{11... | collective-permute-start | bytes 6291464 | tf_op jit(solution)/shard_map/while/body/eval_jaxpr/ppermute | solution.py:15
  418.2 3.3 collective-permute-done.1
  421.6 24.3 %fusion.25 = f32[1,2,16,4,128,128]{5,4,3,2,1,0:T(8,128)S(1)} fusion(f32[1,2,16,4,128,128]{5,4,3,2,1,0:T(8,128)} %copy-done, f32[1,2,16,1,128,128]{5,4,3,2,1,0:T(8,128)} %collective-permute-done, f32[1,2,16,1,128,128]{5,4,3,2,1,0:T(8,128)} %collective-permute-done.1, f32[4,128,128]{2,1,0:T(8,128)} %get-tuple-element.259), kind=kLoop, calls=%fused_computation.8.clone.1 | loop fusion | flops 18874368 | bytes 21233664 | tf_op jit(solution)/shard_map/while/body/eval_jaxpr/sub | solution.py:29
  445.9 7.1 %add_divide_fusion.2 = (f32[1,1,16,4,128,128]{5,4,3,2,1,0:T(8,128)}, f32[1,1,16,4,128,128]{5,4,3,2,1,0:T(8,128)}) fusion(f32[4,128,128]{2,1,0:T(8,128)} %get-tuple-element.258, f32[]{:T(128)} %bitcast.45, f32[4,128,128]{2,1,0:T(8,128)} %get-tuple-element.259, f32[1,2,16,4,128,128]{5,4,3,2,1,0:T(8,128)S(1)} %bitcast.49, ...), kind=kLoop, calls=%fused_computation.22.clone.1 | loop fusion | flops 14680064 | bytes 29884420 | tf_op jit(solution)/shard_map/while/body/eval_jaxpr/div | solution.py:33
  453.0 4.7 fusion.26
  461.0 7.5 %reshape.188 = f32[2,16,65536]{2,1,0:T(8,128)} reshape(f32[1,2,16,4,128,128]{5,4,3,2,1,0:T(8,128)} %get-tuple-element.162) | data formatting | bytes 16777216 | tf_op jit(solution)/shard_map/reshape.4
  468.5 4.0 reshape.196
  472.4 27.3 %fusion.11 = f32[1,16,16]{2,1,0:T(8,128)S(1)} fusion(f32[2,16,4,128,128]{4,3,2,1,0:T(8,128)} %bitcast.52), kind=kOutput, calls=%fused_computation.30 | convolution fusion | flops 402653184 | bytes 8389632 | tf_op jit(solution)/shard_map/naic,najc->nij/dot_general | solution.py:62
  501.0 8.4 %convolution_bitcast_fusion.1 = f32[1,2,16,16]{3,2,1,0:T(8,128)S(1)} fusion(f32[2,16,65536]{2,1,0:T(8,128)S(1)} %copy-done.2, f32[16,65536,1]{1,0,2:T(8,128)} %reshape.196), kind=kOutput, calls=%fused_computation.29 | convolution fusion | flops 402653184 | bytes 12584960 | tf_op jit(solution)/shard_map/naic,pc->naip/dot_general | solution.py:59
  509.4 45.7 %all-reduce.1 = (f32[1,2,16,16]{3,2,1,0:T(8,128)S(1)}, f32[1,16,16]{2,1,0:T(8,128)S(1)}) all-reduce(f32[1,2,16,16]{3,2,1,0:T(8,128)S(1)} %convolution_bitcast_fusion.1, f32[1,16,16]{2,1,0:T(8,128)S(1)} %fusion.11), channel_id=1, replica_groups=mesh['node'=4,'row'=8] {'row'}, use_global_device_ids=true, to_apply=%region_4.5 | all-reduce | flops 768 | bytes 6144 | tf_op jit(solution)/shard_map/psum | solution.py:65
  555.2 8.4 %convolution_bitcast_fusion = f32[16,65536]{1,0:T(8,128)} fusion(f32[2,16,65536]{2,1,0:T(8,128)} %reshape.188, f32[1,2,16,16]{3,2,1,0:T(8,128)S(1)} %get-tuple-element.201, f32[]{:T(128)} %select_reduce_fusion), kind=kOutput, calls=%fused_computation.25 | convolution fusion | flops 402653696 | bytes 12584964 | tf_op jit(solution)/shard_map/naip,naic->pc/dot_general | solution.py:72
  564.8 100.7 %all-reduce.4.cloned.1.call-done = f32[16,65536]{1,0:T(8,128)} async-done(((f32[16,65536]{1,0:T(8,128)}), f32[16,65536]{1,0:T(8,128)}) %all-reduce.4.cloned.1.call-update) | async-done | bytes 4194320 | tf_op jit(solution)/shard_map/psum | solution.py:73
  (130 shorter events, 59.6 us)
Async XLA Ops:
  7.2 658.4 %all-reduce.4.cloned.1.call-start = ((), (), s32[]{:S(2)}) async-start(), calls=%async_computation | async-start | bytes 8388608 | tf_op jit(solution)/shard_map/psum | solution.py:73
  17.5 7.4 %copy-start.3 = (f32[4,128,128]{2,1,0:T(8,128)S(1)}, f32[4,128,128]{2,1,0:T(8,128)}, u32[]{:S(2)}) copy-start(f32[4,128,128]{2,1,0:T(8,128)} %get-tuple-element.285) | copy-start | bytes 786436 | tf_op jit(solution)/shard_map/while
  19.3 6.6 collective-permute-start
  23.0 7.0 %collective-permute-start.1 = (f32[1,2,16,1,128,128]{5,4,3,2,1,0:T(8,128)S(1)}, f32[1,2,16,1,128,128]{5,4,3,2,1,0:T(8,128)}, u32[]{:S(2)}, u32[]{:S(2)}) collective-permute-start(f32[1,2,16,1,128,128]{5,4,3,2,1,0:T(8,128)S(1)} %get-tuple-element.261), channel_id=1, source_target_pairs={{1,0},{2,1},{3,2},{4,3},{5,4},{6,5},{7,6},{9,8},{10,9},{11,10},{12... | collective-permute-start | bytes 6291464 | tf_op jit(solution)/shard_map/while/body/eval_jaxpr/ppermute | solution.py:18
  25.0 29.3 %slice-start = ((s8[8388608]{0:T(1024)(128)(4,1)}), s8[4194304]{0:T(1024)(128)(4,1)S(1)}, s32[]{:S(2)}) async-start(s8[8388608]{0:T(1024)(128)(4,1)} %bitcast.48), calls=%async_computation.1 | async-start | bytes 8388608 | tf_op jit(solution)/shard_map/while
  30.0 24.3 %slice-start.1 = ((s8[8388608]{0:T(1024)(128)(4,1)}), s8[4194304]{0:T(1024)(128)(4,1)S(1)}, s32[]{:S(2)}) async-start(s8[8388608]{0:T(1024)(128)(4,1)} %bitcast.48), calls=%async_computation.2 | async-start | bytes 8388608 | tf_op jit(solution)/shard_map/while
  30.0 31.5 %slice-start.2 = ((s8[8388608]{0:T(1024)(128)(4,1)}), s8[4194304]{0:T(1024)(128)(4,1)S(1)}, s32[]{:S(2)}) async-start(s8[8388608]{0:T(1024)(128)(4,1)} %bitcast.50), calls=%async_computation.3 | async-start | bytes 8388608 | tf_op jit(solution)/shard_map/while
  54.3 7.2 %slice-start.3 = ((s8[8388608]{0:T(1024)(128)(4,1)}), s8[4194304]{0:T(1024)(128)(4,1)S(1)}, s32[]{:S(2)}) async-start(s8[8388608]{0:T(1024)(128)(4,1)} %bitcast.50), calls=%async_computation.4 | async-start | bytes 8388608 | tf_op jit(solution)/shard_map/while
  66.2 3.2 copy-start.1
  76.9 28.7 %copy-start.3 = (f32[4,128,128]{2,1,0:T(8,128)S(1)}, f32[4,128,128]{2,1,0:T(8,128)}, u32[]{:S(2)}) copy-start(f32[4,128,128]{2,1,0:T(8,128)} %get-tuple-element.285) | copy-start | bytes 786436 | tf_op jit(solution)/shard_map/while
  78.6 27.9 %collective-permute-start = (f32[1,2,16,1,128,128]{5,4,3,2,1,0:T(8,128)}, f32[1,2,16,1,128,128]{5,4,3,2,1,0:T(8,128)}, u32[]{:S(2)}, u32[]{:S(2)}) collective-permute-start(f32[1,2,16,1,128,128]{5,4,3,2,1,0:T(8,128)} %get-tuple-element.260), channel_id=1, source_target_pairs={{0,1},{1,2},{2,3},{3,4},{4,5},{5,6},{6,7},{8,9},{9,10},{10,11},{11... | collective-permute-start | bytes 6291464 | tf_op jit(solution)/shard_map/while/body/eval_jaxpr/ppermute | solution.py:15
  103.6 6.2 collective-permute-start.1
  105.6 28.5 %slice-start = ((s8[8388608]{0:T(1024)(128)(4,1)}), s8[4194304]{0:T(1024)(128)(4,1)S(1)}, s32[]{:S(2)}) async-start(s8[8388608]{0:T(1024)(128)(4,1)} %bitcast.48), calls=%async_computation.1 | async-start | bytes 8388608 | tf_op jit(solution)/shard_map/while
  109.8 24.3 %slice-start.1 = ((s8[8388608]{0:T(1024)(128)(4,1)}), s8[4194304]{0:T(1024)(128)(4,1)S(1)}, s32[]{:S(2)}) async-start(s8[8388608]{0:T(1024)(128)(4,1)} %bitcast.48), calls=%async_computation.2 | async-start | bytes 8388608 | tf_op jit(solution)/shard_map/while
  109.8 31.5 %slice-start.2 = ((s8[8388608]{0:T(1024)(128)(4,1)}), s8[4194304]{0:T(1024)(128)(4,1)S(1)}, s32[]{:S(2)}) async-start(s8[8388608]{0:T(1024)(128)(4,1)} %bitcast.50), calls=%async_computation.3 | async-start | bytes 8388608 | tf_op jit(solution)/shard_map/while
  134.1 7.2 %slice-start.3 = ((s8[8388608]{0:T(1024)(128)(4,1)}), s8[4194304]{0:T(1024)(128)(4,1)S(1)}, s32[]{:S(2)}) async-start(s8[8388608]{0:T(1024)(128)(4,1)} %bitcast.50), calls=%async_computation.4 | async-start | bytes 8388608 | tf_op jit(solution)/shard_map/while
  156.6 26.9 %copy-start.3 = (f32[4,128,128]{2,1,0:T(8,128)S(1)}, f32[4,128,128]{2,1,0:T(8,128)}, u32[]{:S(2)}) copy-start(f32[4,128,128]{2,1,0:T(8,128)} %get-tuple-element.285) | copy-start | bytes 786436 | tf_op jit(solution)/shard_map/while
  158.3 26.0 %collective-permute-start = (f32[1,2,16,1,128,128]{5,4,3,2,1,0:T(8,128)}, f32[1,2,16,1,128,128]{5,4,3,2,1,0:T(8,128)}, u32[]{:S(2)}, u32[]{:S(2)}) collective-permute-start(f32[1,2,16,1,128,128]{5,4,3,2,1,0:T(8,128)} %get-tuple-element.260), channel_id=1, source_target_pairs={{0,1},{1,2},{2,3},{3,4},{4,5},{5,6},{6,7},{8,9},{9,10},{10,11},{11... | collective-permute-start | bytes 6291464 | tf_op jit(solution)/shard_map/while/body/eval_jaxpr/ppermute | solution.py:15
  181.5 6.2 collective-permute-start.1
  183.5 28.5 %slice-start = ((s8[8388608]{0:T(1024)(128)(4,1)}), s8[4194304]{0:T(1024)(128)(4,1)S(1)}, s32[]{:S(2)}) async-start(s8[8388608]{0:T(1024)(128)(4,1)} %bitcast.48), calls=%async_computation.1 | async-start | bytes 8388608 | tf_op jit(solution)/shard_map/while
  187.7 24.3 %slice-start.1 = ((s8[8388608]{0:T(1024)(128)(4,1)}), s8[4194304]{0:T(1024)(128)(4,1)S(1)}, s32[]{:S(2)}) async-start(s8[8388608]{0:T(1024)(128)(4,1)} %bitcast.48), calls=%async_computation.2 | async-start | bytes 8388608 | tf_op jit(solution)/shard_map/while
  187.7 31.5 %slice-start.2 = ((s8[8388608]{0:T(1024)(128)(4,1)}), s8[4194304]{0:T(1024)(128)(4,1)S(1)}, s32[]{:S(2)}) async-start(s8[8388608]{0:T(1024)(128)(4,1)} %bitcast.50), calls=%async_computation.3 | async-start | bytes 8388608 | tf_op jit(solution)/shard_map/while
  212.0 7.2 %slice-start.3 = ((s8[8388608]{0:T(1024)(128)(4,1)}), s8[4194304]{0:T(1024)(128)(4,1)S(1)}, s32[]{:S(2)}) async-start(s8[8388608]{0:T(1024)(128)(4,1)} %bitcast.50), calls=%async_computation.4 | async-start | bytes 8388608 | tf_op jit(solution)/shard_map/while
  223.9 3.2 copy-start.1
  234.6 26.9 %copy-start.3 = (f32[4,128,128]{2,1,0:T(8,128)S(1)}, f32[4,128,128]{2,1,0:T(8,128)}, u32[]{:S(2)}) copy-start(f32[4,128,128]{2,1,0:T(8,128)} %get-tuple-element.285) | copy-start | bytes 786436 | tf_op jit(solution)/shard_map/while
  236.3 26.0 %collective-permute-start = (f32[1,2,16,1,128,128]{5,4,3,2,1,0:T(8,128)}, f32[1,2,16,1,128,128]{5,4,3,2,1,0:T(8,128)}, u32[]{:S(2)}, u32[]{:S(2)}) collective-permute-start(f32[1,2,16,1,128,128]{5,4,3,2,1,0:T(8,128)} %get-tuple-element.260), channel_id=1, source_target_pairs={{0,1},{1,2},{2,3},{3,4},{4,5},{5,6},{6,7},{8,9},{9,10},{10,11},{11... | collective-permute-start | bytes 6291464 | tf_op jit(solution)/shard_map/while/body/eval_jaxpr/ppermute | solution.py:15
  259.5 6.2 collective-permute-start.1
  261.5 28.5 %slice-start = ((s8[8388608]{0:T(1024)(128)(4,1)}), s8[4194304]{0:T(1024)(128)(4,1)S(1)}, s32[]{:S(2)}) async-start(s8[8388608]{0:T(1024)(128)(4,1)} %bitcast.48), calls=%async_computation.1 | async-start | bytes 8388608 | tf_op jit(solution)/shard_map/while
  265.7 24.3 %slice-start.1 = ((s8[8388608]{0:T(1024)(128)(4,1)}), s8[4194304]{0:T(1024)(128)(4,1)S(1)}, s32[]{:S(2)}) async-start(s8[8388608]{0:T(1024)(128)(4,1)} %bitcast.48), calls=%async_computation.2 | async-start | bytes 8388608 | tf_op jit(solution)/shard_map/while
  265.7 31.5 %slice-start.2 = ((s8[8388608]{0:T(1024)(128)(4,1)}), s8[4194304]{0:T(1024)(128)(4,1)S(1)}, s32[]{:S(2)}) async-start(s8[8388608]{0:T(1024)(128)(4,1)} %bitcast.50), calls=%async_computation.3 | async-start | bytes 8388608 | tf_op jit(solution)/shard_map/while
  290.0 7.2 %slice-start.3 = ((s8[8388608]{0:T(1024)(128)(4,1)}), s8[4194304]{0:T(1024)(128)(4,1)S(1)}, s32[]{:S(2)}) async-start(s8[8388608]{0:T(1024)(128)(4,1)} %bitcast.50), calls=%async_computation.4 | async-start | bytes 8388608 | tf_op jit(solution)/shard_map/while
  301.8 3.2 copy-start.1
  312.5 26.9 %copy-start.3 = (f32[4,128,128]{2,1,0:T(8,128)S(1)}, f32[4,128,128]{2,1,0:T(8,128)}, u32[]{:S(2)}) copy-start(f32[4,128,128]{2,1,0:T(8,128)} %get-tuple-element.285) | copy-start | bytes 786436 | tf_op jit(solution)/shard_map/while
  314.2 26.0 %collective-permute-start = (f32[1,2,16,1,128,128]{5,4,3,2,1,0:T(8,128)}, f32[1,2,16,1,128,128]{5,4,3,2,1,0:T(8,128)}, u32[]{:S(2)}, u32[]{:S(2)}) collective-permute-start(f32[1,2,16,1,128,128]{5,4,3,2,1,0:T(8,128)} %get-tuple-element.260), channel_id=1, source_target_pairs={{0,1},{1,2},{2,3},{3,4},{4,5},{5,6},{6,7},{8,9},{9,10},{10,11},{11... | collective-permute-start | bytes 6291464 | tf_op jit(solution)/shard_map/while/body/eval_jaxpr/ppermute | solution.py:15
  337.4 6.2 collective-permute-start.1
  339.4 28.5 %slice-start = ((s8[8388608]{0:T(1024)(128)(4,1)}), s8[4194304]{0:T(1024)(128)(4,1)S(1)}, s32[]{:S(2)}) async-start(s8[8388608]{0:T(1024)(128)(4,1)} %bitcast.48), calls=%async_computation.1 | async-start | bytes 8388608 | tf_op jit(solution)/shard_map/while
  343.6 24.3 %slice-start.1 = ((s8[8388608]{0:T(1024)(128)(4,1)}), s8[4194304]{0:T(1024)(128)(4,1)S(1)}, s32[]{:S(2)}) async-start(s8[8388608]{0:T(1024)(128)(4,1)} %bitcast.48), calls=%async_computation.2 | async-start | bytes 8388608 | tf_op jit(solution)/shard_map/while
  343.6 31.5 %slice-start.2 = ((s8[8388608]{0:T(1024)(128)(4,1)}), s8[4194304]{0:T(1024)(128)(4,1)S(1)}, s32[]{:S(2)}) async-start(s8[8388608]{0:T(1024)(128)(4,1)} %bitcast.50), calls=%async_computation.3 | async-start | bytes 8388608 | tf_op jit(solution)/shard_map/while
  367.9 7.2 %slice-start.3 = ((s8[8388608]{0:T(1024)(128)(4,1)}), s8[4194304]{0:T(1024)(128)(4,1)S(1)}, s32[]{:S(2)}) async-start(s8[8388608]{0:T(1024)(128)(4,1)} %bitcast.50), calls=%async_computation.4 | async-start | bytes 8388608 | tf_op jit(solution)/shard_map/while
  390.5 26.9 %copy-start.3 = (f32[4,128,128]{2,1,0:T(8,128)S(1)}, f32[4,128,128]{2,1,0:T(8,128)}, u32[]{:S(2)}) copy-start(f32[4,128,128]{2,1,0:T(8,128)} %get-tuple-element.285) | copy-start | bytes 786436 | tf_op jit(solution)/shard_map/while
  392.2 26.0 %collective-permute-start = (f32[1,2,16,1,128,128]{5,4,3,2,1,0:T(8,128)}, f32[1,2,16,1,128,128]{5,4,3,2,1,0:T(8,128)}, u32[]{:S(2)}, u32[]{:S(2)}) collective-permute-start(f32[1,2,16,1,128,128]{5,4,3,2,1,0:T(8,128)} %get-tuple-element.260), channel_id=1, source_target_pairs={{0,1},{1,2},{2,3},{3,4},{4,5},{5,6},{6,7},{8,9},{9,10},{10,11},{11... | collective-permute-start | bytes 6291464 | tf_op jit(solution)/shard_map/while/body/eval_jaxpr/ppermute | solution.py:15
  415.4 6.2 collective-permute-start.1
  417.4 28.5 %slice-start = ((s8[8388608]{0:T(1024)(128)(4,1)}), s8[4194304]{0:T(1024)(128)(4,1)S(1)}, s32[]{:S(2)}) async-start(s8[8388608]{0:T(1024)(128)(4,1)} %bitcast.48), calls=%async_computation.1 | async-start | bytes 8388608 | tf_op jit(solution)/shard_map/while
  421.6 24.3 %slice-start.1 = ((s8[8388608]{0:T(1024)(128)(4,1)}), s8[4194304]{0:T(1024)(128)(4,1)S(1)}, s32[]{:S(2)}) async-start(s8[8388608]{0:T(1024)(128)(4,1)} %bitcast.48), calls=%async_computation.2 | async-start | bytes 8388608 | tf_op jit(solution)/shard_map/while
  421.6 31.5 %slice-start.2 = ((s8[8388608]{0:T(1024)(128)(4,1)}), s8[4194304]{0:T(1024)(128)(4,1)S(1)}, s32[]{:S(2)}) async-start(s8[8388608]{0:T(1024)(128)(4,1)} %bitcast.50), calls=%async_computation.3 | async-start | bytes 8388608 | tf_op jit(solution)/shard_map/while
  445.9 7.2 %slice-start.3 = ((s8[8388608]{0:T(1024)(128)(4,1)}), s8[4194304]{0:T(1024)(128)(4,1)S(1)}, s32[]{:S(2)}) async-start(s8[8388608]{0:T(1024)(128)(4,1)} %bitcast.50), calls=%async_computation.4 | async-start | bytes 8388608 | tf_op jit(solution)/shard_map/while
  468.5 31.3 %copy-start.4 = (f32[4]{0:T(128)S(1)}, f32[4]{0:T(128)}, u32[]{:S(2)}) copy-start(f32[4]{0:T(128)} %param.13) | copy-start | bytes 52
  472.4 28.5 %copy-start.2 = (f32[2,16,65536]{2,1,0:T(8,128)S(1)}, f32[2,16,65536]{2,1,0:T(8,128)}, u32[]{:S(2)}) copy-start(f32[2,16,65536]{2,1,0:T(8,128)} %reshape.188) | copy-start | bytes 25165828
  (9 other events, 29.1 us)
Sparse Core Ops, SparseCore 0:
  563.7 101.8 all-reduce.3
where the time goes:
time: 678 us
  other arithmetic  252 us (37%)
  starting transfers between devices  129 us (19%)
  waiting for transfers between devices  122 us (18%)
  local copies, waits for them, and re-layouts  64.7 us (10%)
  blocking collectives  45.7 us (7%)
  matrix products  44.1 us (7%)
  between operations  15.2 us (2%)
    sub x6, other arithmetic, relax_step(): applied = diag_full * fields - beside  146 us
    ppermute x6, starting transfers between devices, with_halo(): lax.ppermute(lax.slice_in_dim(block, block.shape[dim] - width, None, axis...  122 us
    psum x1, waiting for transfers between devices, local(): summed = lax.psum(share, 'node')  101 us
    psum x1, blocking collectives, local(): projected, gram_part = lax.psum((projected, gram_part), 'row')  45.7 us
    div x6, other arithmetic, relax_step(): step_real = (diag_full * resid_real + shift_col * resid_imag) / denominator  42.9 us
    while x84, local copies, waits for them, and re-layouts  38.8 us
    add x6, other arithmetic, relax_step(): return fields + active * jnp.stack([step_real, step_imag], 1)  28 us
    dot_general x1, matrix products, local(): jnp.einsum('naic,najc->nij', flat_fields, flat_fields, precision=lax.Prec...  27.3 us
  transfers between devices with their start and end apart: 13, of which 7 were waited for; matrix products, arithmetic and copies ran while one was open for 1% of the time, Pallas kernels for 0%

commit v1 on v0

--- a/solution.py
+++ b/solution.py
@@ -5,6 +5,14 @@
 
 NODE_DEV = 1
 ITERS = 6
+
+
+def add_in_pairs(x, axis):
+    size, result = (lax.axis_size(axis), x)
+    for reach in [1 << k for k in range(size.bit_length() - 1)]:
+        route = [(i, i ^ reach) for i in range(size)]
+        result = result + lax.ppermute(result, axis, route)
+    return result
 
 
 def with_halo(block, sides, width):
@@ -70,7 +78,7 @@
     )
     weighted = projected * my_weights.reshape(NODE_DEV, 1, 1, 1)
     share = jnp.einsum("naip,naic->pc", weighted, flat_fields, precision=lax.Precision.HIGHEST)
-    summed = lax.psum(share, "node")
+    summed = add_in_pairs(share, "node")
     probe_response = (summed / quad_count).reshape(observations.shape)
     return (probe_response, group_gram[None])
 

time: 678 us -> 747 us (1.10)
  waiting for transfers between devices: 122 us -> 200 us
  between operations: 15.2 us -> 1.95 us
    ppermute x0 -> x2, waiting for transfers between devices: none -> 173 us  [add_in_pairs(): result = result + lax.ppermute(result, axis, route)]
    psum x1 -> x0, waiting for transfers between devices: 101 us -> none  [local(): summed = lax.psum(share, 'node')]
  transfers between devices with their start and end apart: 13 -> 14, of which waited for: 7 -> 14; matrix products, arithmetic and copies ran while one was open for 1% -> 0% of each run, Pallas kernels for 0% -> 0%
where the time goes in v1:
time: 747 us; the launch traced here: 744 us
  other arithmetic  255 us (34%)
  waiting for transfers between devices  200 us (27%)
  starting transfers between devices  132 us (18%)
  local copies, waits for them, and re-layouts  61.8 us (8%)
  blocking collectives  45.8 us (6%)
  matrix products  43.1 us (6%)
    ppermute x2, waiting for transfers between devices, add_in_pairs(): result = result + lax.ppermute(result, axis, route)  173 us
    sub x6, other arithmetic, relax_step(): applied = diag_full * fields - beside  144 us
    ppermute x6, starting transfers between devices, with_halo(): lax.ppermute(lax.slice_in_dim(block, block.shape[dim] - width, None, axis...  122 us
    div x6, other arithmetic, relax_step(): step_real = (diag_full * resid_real + shift_col * resid_imag) / denominator  49.2 us
    psum x1, blocking collectives, local(): projected, gram_part = lax.psum((projected, gram_part), 'row')  45.8 us
    add x6, other arithmetic, relax_step(): return fields + active * jnp.stack([step_real, step_imag], 1)  32.2 us
    while x84, local copies, waits for them, and re-layouts  31.7 us
    dot_general x1, matrix products, local(): jnp.einsum('naic,najc->nij', flat_fields, flat_fields, precision=lax.Prec...  27.4 us
  transfers between devices with their start and end apart: 14, of which 14 were waited for; matrix products, arithmetic and copies ran while one was open for 0% of the time, Pallas kernels for 0%

profile of v1, /device:TPU:0, one launch (start us, length us, event | category | flops | bytes accessed | tf_op | source)
XLA Modules:
  0.0 744.0 jit_solution(18044328120440762440)
XLA Ops:
  7.1 454.6 %while.16 = (s32[]{:T(128)}, f32[1,2,16,4,128,128]{5,4,3,2,1,0:T(8,128)}, s32[1]{0:T(128)}, f32[4,128,128]{2,1,0:T(8,128)}, f32[16,4,128,128]{3,2,1,0:T(8,128)},...) while((s32[]{:T(128)}, ...), condition=%wide.region_3.4_spmd.clone, body=%wide.region_2.3_spmd.clone.sunk | while | flops 44236800 | bytes 237502864 | solution.py:63
  12.4 3.7 collective-permute-start
  18.9 4.5 collective-permute-done.1
  23.4 23.9 %fusion.25 = f32[1,2,16,4,128,128]{5,4,3,2,1,0:T(8,128)S(1)} fusion(f32[1,2,16,4,128,128]{5,4,3,2,1,0:T(8,128)} %copy-done, f32[1,2,16,1,128,128]{5,4,3,2,1,0:T(8,128)} %collective-permute-done, f32[1,2,16,1,128,128]{5,4,3,2,1,0:T(8,128)} %collective-permute-done.1, f32[4,128,128]{2,1,0:T(8,128)S(1)} %get-tuple-element.259), kind=kLoop, calls=%fused_computation.8.clone.1 | loop fusion | flops 18874368 | bytes 21233664 | tf_op jit(solution)/shard_map/while/body/eval_jaxpr/sub | solution.py:37
  47.4 8.2 %add_divide_fusion.2 = (f32[1,1,16,4,128,128]{5,4,3,2,1,0:T(8,128)}, f32[1,1,16,4,128,128]{5,4,3,2,1,0:T(8,128)}) fusion(f32[4,128,128]{2,1,0:T(8,128)S(1)} %get-tuple-element.258, f32[]{:T(128)} %bitcast.45, f32[4,128,128]{2,1,0:T(8,128)S(1)} %get-tuple-element.259, f32[1,2,16,4,128,128]{5,4,3,2,1,0:T(8,128)S(1)} %bitcast.49, ...), kind=kLoop, calls=%fused_computation.22.clone.1 | loop fusion | flops 14680064 | bytes 29884420 | tf_op jit(solution)/shard_map/while/body/eval_jaxpr/div | solution.py:41
  55.6 5.4 fusion.26
  61.0 3.2 copy-done.1
  64.2 4.2 broadcast_select_fusion.2
  72.9 25.0 %collective-permute-start = (f32[1,2,16,1,128,128]{5,4,3,2,1,0:T(8,128)}, f32[1,2,16,1,128,128]{5,4,3,2,1,0:T(8,128)}, u32[]{:S(2)}, u32[]{:S(2)}) collective-permute-start(f32[1,2,16,1,128,128]{5,4,3,2,1,0:T(8,128)} %get-tuple-element.260), channel_id=1, source_target_pairs={{0,1},{1,2},{2,3},{3,4},{4,5},{5,6},{6,7},{8,9},{9,10},{10,11},{11... | collective-permute-start | bytes 6291464 | tf_op jit(solution)/shard_map/while/body/eval_jaxpr/ppermute | solution.py:23
  100.7 3.6 collective-permute-done.1
  104.3 23.9 %fusion.25 = f32[1,2,16,4,128,128]{5,4,3,2,1,0:T(8,128)S(1)} fusion(f32[1,2,16,4,128,128]{5,4,3,2,1,0:T(8,128)} %copy-done, f32[1,2,16,1,128,128]{5,4,3,2,1,0:T(8,128)} %collective-permute-done, f32[1,2,16,1,128,128]{5,4,3,2,1,0:T(8,128)} %collective-permute-done.1, f32[4,128,128]{2,1,0:T(8,128)S(1)} %get-tuple-element.259), kind=kLoop, calls=%fused_computation.8.clone.1 | loop fusion | flops 18874368 | bytes 21233664 | tf_op jit(solution)/shard_map/while/body/eval_jaxpr/sub | solution.py:37
  128.3 8.2 %add_divide_fusion.2 = (f32[1,1,16,4,128,128]{5,4,3,2,1,0:T(8,128)}, f32[1,1,16,4,128,128]{5,4,3,2,1,0:T(8,128)}) fusion(f32[4,128,128]{2,1,0:T(8,128)S(1)} %get-tuple-element.258, f32[]{:T(128)} %bitcast.45, f32[4,128,128]{2,1,0:T(8,128)S(1)} %get-tuple-element.259, f32[1,2,16,4,128,128]{5,4,3,2,1,0:T(8,128)S(1)} %bitcast.49, ...), kind=kLoop, calls=%fused_computation.22.clone.1 | loop fusion | flops 14680064 | bytes 29884420 | tf_op jit(solution)/shard_map/while/body/eval_jaxpr/div | solution.py:41
  136.5 5.4 fusion.26
  141.9 3.2 copy-done.1
  145.1 4.2 broadcast_select_fusion.2
  153.9 23.2 %collective-permute-start = (f32[1,2,16,1,128,128]{5,4,3,2,1,0:T(8,128)}, f32[1,2,16,1,128,128]{5,4,3,2,1,0:T(8,128)}, u32[]{:S(2)}, u32[]{:S(2)}) collective-permute-start(f32[1,2,16,1,128,128]{5,4,3,2,1,0:T(8,128)} %get-tuple-element.260), channel_id=1, source_target_pairs={{0,1},{1,2},{2,3},{3,4},{4,5},{5,6},{6,7},{8,9},{9,10},{10,11},{11... | collective-permute-start | bytes 6291464 | tf_op jit(solution)/shard_map/while/body/eval_jaxpr/ppermute | solution.py:23
  179.8 3.6 collective-permute-done.1
  183.5 23.9 %fusion.25 = f32[1,2,16,4,128,128]{5,4,3,2,1,0:T(8,128)S(1)} fusion(f32[1,2,16,4,128,128]{5,4,3,2,1,0:T(8,128)} %copy-done, f32[1,2,16,1,128,128]{5,4,3,2,1,0:T(8,128)} %collective-permute-done, f32[1,2,16,1,128,128]{5,4,3,2,1,0:T(8,128)} %collective-permute-done.1, f32[4,128,128]{2,1,0:T(8,128)S(1)} %get-tuple-element.259), kind=kLoop, calls=%fused_computation.8.clone.1 | loop fusion | flops 18874368 | bytes 21233664 | tf_op jit(solution)/shard_map/while/body/eval_jaxpr/sub | solution.py:37
  207.5 8.2 %add_divide_fusion.2 = (f32[1,1,16,4,128,128]{5,4,3,2,1,0:T(8,128)}, f32[1,1,16,4,128,128]{5,4,3,2,1,0:T(8,128)}) fusion(f32[4,128,128]{2,1,0:T(8,128)S(1)} %get-tuple-element.258, f32[]{:T(128)} %bitcast.45, f32[4,128,128]{2,1,0:T(8,128)S(1)} %get-tuple-element.259, f32[1,2,16,4,128,128]{5,4,3,2,1,0:T(8,128)S(1)} %bitcast.49, ...), kind=kLoop, calls=%fused_computation.22.clone.1 | loop fusion | flops 14680064 | bytes 29884420 | tf_op jit(solution)/shard_map/while/body/eval_jaxpr/div | solution.py:41
  215.7 5.4 fusion.26
  221.1 3.2 copy-done.1
  224.3 4.2 broadcast_select_fusion.2
  233.0 23.2 %collective-permute-start = (f32[1,2,16,1,128,128]{5,4,3,2,1,0:T(8,128)}, f32[1,2,16,1,128,128]{5,4,3,2,1,0:T(8,128)}, u32[]{:S(2)}, u32[]{:S(2)}) collective-permute-start(f32[1,2,16,1,128,128]{5,4,3,2,1,0:T(8,128)} %get-tuple-element.260), channel_id=1, source_target_pairs={{0,1},{1,2},{2,3},{3,4},{4,5},{5,6},{6,7},{8,9},{9,10},{10,11},{11... | collective-permute-start | bytes 6291464 | tf_op jit(solution)/shard_map/while/body/eval_jaxpr/ppermute | solution.py:23
  259.0 3.6 collective-permute-done.1
  262.6 23.9 %fusion.25 = f32[1,2,16,4,128,128]{5,4,3,2,1,0:T(8,128)S(1)} fusion(f32[1,2,16,4,128,128]{5,4,3,2,1,0:T(8,128)} %copy-done, f32[1,2,16,1,128,128]{5,4,3,2,1,0:T(8,128)} %collective-permute-done, f32[1,2,16,1,128,128]{5,4,3,2,1,0:T(8,128)} %collective-permute-done.1, f32[4,128,128]{2,1,0:T(8,128)S(1)} %get-tuple-element.259), kind=kLoop, calls=%fused_computation.8.clone.1 | loop fusion | flops 18874368 | bytes 21233664 | tf_op jit(solution)/shard_map/while/body/eval_jaxpr/sub | solution.py:37
  286.6 8.2 %add_divide_fusion.2 = (f32[1,1,16,4,128,128]{5,4,3,2,1,0:T(8,128)}, f32[1,1,16,4,128,128]{5,4,3,2,1,0:T(8,128)}) fusion(f32[4,128,128]{2,1,0:T(8,128)S(1)} %get-tuple-element.258, f32[]{:T(128)} %bitcast.45, f32[4,128,128]{2,1,0:T(8,128)S(1)} %get-tuple-element.259, f32[1,2,16,4,128,128]{5,4,3,2,1,0:T(8,128)S(1)} %bitcast.49, ...), kind=kLoop, calls=%fused_computation.22.clone.1 | loop fusion | flops 14680064 | bytes 29884420 | tf_op jit(solution)/shard_map/while/body/eval_jaxpr/div | solution.py:41
  294.8 5.4 fusion.26
  300.2 3.2 copy-done.1
  303.4 4.2 broadcast_select_fusion.2
  312.1 23.2 %collective-permute-start = (f32[1,2,16,1,128,128]{5,4,3,2,1,0:T(8,128)}, f32[1,2,16,1,128,128]{5,4,3,2,1,0:T(8,128)}, u32[]{:S(2)}, u32[]{:S(2)}) collective-permute-start(f32[1,2,16,1,128,128]{5,4,3,2,1,0:T(8,128)} %get-tuple-element.260), channel_id=1, source_target_pairs={{0,1},{1,2},{2,3},{3,4},{4,5},{5,6},{6,7},{8,9},{9,10},{10,11},{11... | collective-permute-start | bytes 6291464 | tf_op jit(solution)/shard_map/while/body/eval_jaxpr/ppermute | solution.py:23
  338.1 3.6 collective-permute-done.1
  341.7 23.9 %fusion.25 = f32[1,2,16,4,128,128]{5,4,3,2,1,0:T(8,128)S(1)} fusion(f32[1,2,16,4,128,128]{5,4,3,2,1,0:T(8,128)} %copy-done, f32[1,2,16,1,128,128]{5,4,3,2,1,0:T(8,128)} %collective-permute-done, f32[1,2,16,1,128,128]{5,4,3,2,1,0:T(8,128)} %collective-permute-done.1, f32[4,128,128]{2,1,0:T(8,128)S(1)} %get-tuple-element.259), kind=kLoop, calls=%fused_computation.8.clone.1 | loop fusion | flops 18874368 | bytes 21233664 | tf_op jit(solution)/shard_map/while/body/eval_jaxpr/sub | solution.py:37
  365.7 8.2 %add_divide_fusion.2 = (f32[1,1,16,4,128,128]{5,4,3,2,1,0:T(8,128)}, f32[1,1,16,4,128,128]{5,4,3,2,1,0:T(8,128)}) fusion(f32[4,128,128]{2,1,0:T(8,128)S(1)} %get-tuple-element.258, f32[]{:T(128)} %bitcast.45, f32[4,128,128]{2,1,0:T(8,128)S(1)} %get-tuple-element.259, f32[1,2,16,4,128,128]{5,4,3,2,1,0:T(8,128)S(1)} %bitcast.49, ...), kind=kLoop, calls=%fused_computation.22.clone.1 | loop fusion | flops 14680064 | bytes 29884420 | tf_op jit(solution)/shard_map/while/body/eval_jaxpr/div | solution.py:41
  373.9 5.4 fusion.26
  382.6 4.2 broadcast_select_fusion.2
  391.3 23.2 %collective-permute-start = (f32[1,2,16,1,128,128]{5,4,3,2,1,0:T(8,128)}, f32[1,2,16,1,128,128]{5,4,3,2,1,0:T(8,128)}, u32[]{:S(2)}, u32[]{:S(2)}) collective-permute-start(f32[1,2,16,1,128,128]{5,4,3,2,1,0:T(8,128)} %get-tuple-element.260), channel_id=1, source_target_pairs={{0,1},{1,2},{2,3},{3,4},{4,5},{5,6},{6,7},{8,9},{9,10},{10,11},{11... | collective-permute-start | bytes 6291464 | tf_op jit(solution)/shard_map/while/body/eval_jaxpr/ppermute | solution.py:23
  417.3 3.6 collective-permute-done.1
  420.9 23.9 %fusion.25 = f32[1,2,16,4,128,128]{5,4,3,2,1,0:T(8,128)S(1)} fusion(f32[1,2,16,4,128,128]{5,4,3,2,1,0:T(8,128)} %copy-done, f32[1,2,16,1,128,128]{5,4,3,2,1,0:T(8,128)} %collective-permute-done, f32[1,2,16,1,128,128]{5,4,3,2,1,0:T(8,128)} %collective-permute-done.1, f32[4,128,128]{2,1,0:T(8,128)S(1)} %get-tuple-element.259), kind=kLoop, calls=%fused_computation.8.clone.1 | loop fusion | flops 18874368 | bytes 21233664 | tf_op jit(solution)/shard_map/while/body/eval_jaxpr/sub | solution.py:37
  444.9 8.2 %add_divide_fusion.2 = (f32[1,1,16,4,128,128]{5,4,3,2,1,0:T(8,128)}, f32[1,1,16,4,128,128]{5,4,3,2,1,0:T(8,128)}) fusion(f32[4,128,128]{2,1,0:T(8,128)S(1)} %get-tuple-element.258, f32[]{:T(128)} %bitcast.45, f32[4,128,128]{2,1,0:T(8,128)S(1)} %get-tuple-element.259, f32[1,2,16,4,128,128]{5,4,3,2,1,0:T(8,128)S(1)} %bitcast.49, ...), kind=kLoop, calls=%fused_computation.22.clone.1 | loop fusion | flops 14680064 | bytes 29884420 | tf_op jit(solution)/shard_map/while/body/eval_jaxpr/div | solution.py:41
  453.1 5.4 fusion.26
  461.7 7.5 %reshape.188 = f32[2,16,65536]{2,1,0:T(8,128)} reshape(f32[1,2,16,4,128,128]{5,4,3,2,1,0:T(8,128)} %get-tuple-element.162) | data formatting | bytes 16777216 | tf_op jit(solution)/shard_map/reshape.4
  469.2 4.0 reshape.196
  473.2 27.4 %fusion.11 = f32[1,16,16]{2,1,0:T(8,128)S(1)} fusion(f32[2,16,4,128,128]{4,3,2,1,0:T(8,128)} %bitcast.52), kind=kOutput, calls=%fused_computation.30 | convolution fusion | flops 402653184 | bytes 8389632 | tf_op jit(solution)/shard_map/naic,najc->nij/dot_general | solution.py:70
  501.9 8.4 %convolution_bitcast_fusion.1 = f32[1,2,16,16]{3,2,1,0:T(8,128)S(1)} fusion(f32[2,16,65536]{2,1,0:T(8,128)S(1)} %copy-done.2, f32[16,65536,1]{1,0,2:T(8,128)} %reshape.196), kind=kOutput, calls=%fused_computation.29 | convolution fusion | flops 402653184 | bytes 12584960 | tf_op jit(solution)/shard_map/naic,pc->naip/dot_general | solution.py:67
  510.3 45.8 %all-reduce.1 = (f32[1,2,16,16]{3,2,1,0:T(8,128)S(1)}, f32[1,16,16]{2,1,0:T(8,128)S(1)}) all-reduce(f32[1,2,16,16]{3,2,1,0:T(8,128)S(1)} %convolution_bitcast_fusion.1, f32[1,16,16]{2,1,0:T(8,128)S(1)} %fusion.11), channel_id=1, replica_groups=mesh['node'=4,'row'=8] {'row'}, use_global_device_ids=true, to_apply=%region_4.5 | all-reduce | flops 768 | bytes 6144 | tf_op jit(solution)/shard_map/psum | solution.py:73
  556.1 7.2 convolution_bitcast_fusion
  564.9 87.4 %collective-permute-done.2 = f32[16,65536]{1,0:T(8,128)S(1)} collective-permute-done((f32[16,65536]{1,0:T(8,128)S(1)}, f32[16,65536]{1,0:T(8,128)S(1)}, u32[]{:S(2)}, u32[]{:S(2)}) %collective-permute-start.2) | collective-permute-done | bytes 4194336 | tf_op jit(solution)/shard_map/ppermute | solution.py:14
  655.5 85.3 %collective-permute-done.3 = f32[16,65536]{1,0:T(8,128)S(1)} collective-permute-done((f32[16,65536]{1,0:T(8,128)S(1)}, f32[16,65536]{1,0:T(8,128)S(1)}, u32[]{:S(2)}, u32[]{:S(2)}) %collective-permute-start.3) | collective-permute-done | bytes 4194336 | tf_op jit(solution)/shard_map/ppermute | solution.py:14
  (132 shorter events, 61.5 us)
Async XLA Ops:
  7.9 4.5 copy-start
  7.9 10.1 %copy-start.3 = (f32[4,128,128]{2,1,0:T(8,128)S(1)}, f32[4,128,128]{2,1,0:T(8,128)}, u32[]{:S(2)}) copy-start(f32[4,128,128]{2,1,0:T(8,128)} %get-tuple-element.285) | copy-start | bytes 786436 | tf_op jit(solution)/shard_map/while
  12.4 6.5 collective-permute-start
  16.1 7.3 collective-permute-start.1
  23.4 24.0 %slice-start = ((s8[8388608]{0:T(1024)(128)(4,1)}), s8[4194304]{0:T(1024)(128)(4,1)S(1)}, s32[]{:S(2)}) async-start(s8[8388608]{0:T(1024)(128)(4,1)} %bitcast.48), calls=%async_computation | async-start | bytes 8388608 | tf_op jit(solution)/shard_map/while
  23.4 24.0 %slice-start.1 = ((s8[8388608]{0:T(1024)(128)(4,1)}), s8[4194304]{0:T(1024)(128)(4,1)S(1)}, s32[]{:S(2)}) async-start(s8[8388608]{0:T(1024)(128)(4,1)} %bitcast.48), calls=%async_computation.1 | async-start | bytes 8388608 | tf_op jit(solution)/shard_map/while
  47.3 8.3 %slice-start.2 = ((s8[8388608]{0:T(1024)(128)(4,1)}), s8[4194304]{0:T(1024)(128)(4,1)S(1)}, s32[]{:S(2)}) async-start(s8[8388608]{0:T(1024)(128)(4,1)} %bitcast.50), calls=%async_computation.2 | async-start | bytes 8388608 | tf_op jit(solution)/shard_map/while
  47.4 8.2 %slice-start.3 = ((s8[8388608]{0:T(1024)(128)(4,1)}), s8[4194304]{0:T(1024)(128)(4,1)S(1)}, s32[]{:S(2)}) async-start(s8[8388608]{0:T(1024)(128)(4,1)} %bitcast.50), calls=%async_computation.3 | async-start | bytes 8388608 | tf_op jit(solution)/shard_map/while
  68.5 4.5 copy-start
  68.5 31.4 %copy-start.3 = (f32[4,128,128]{2,1,0:T(8,128)S(1)}, f32[4,128,128]{2,1,0:T(8,128)}, u32[]{:S(2)}) copy-start(f32[4,128,128]{2,1,0:T(8,128)} %get-tuple-element.285) | copy-start | bytes 786436 | tf_op jit(solution)/shard_map/while
  72.9 27.8 %collective-permute-start = (f32[1,2,16,1,128,128]{5,4,3,2,1,0:T(8,128)}, f32[1,2,16,1,128,128]{5,4,3,2,1,0:T(8,128)}, u32[]{:S(2)}, u32[]{:S(2)}) collective-permute-start(f32[1,2,16,1,128,128]{5,4,3,2,1,0:T(8,128)} %get-tuple-element.260), channel_id=1, source_target_pairs={{0,1},{1,2},{2,3},{3,4},{4,5},{5,6},{6,7},{8,9},{9,10},{10,11},{11... | collective-permute-start | bytes 6291464 | tf_op jit(solution)/shard_map/while/body/eval_jaxpr/ppermute | solution.py:23
  97.9 6.4 collective-permute-start.1
  104.3 24.0 %slice-start = ((s8[8388608]{0:T(1024)(128)(4,1)}), s8[4194304]{0:T(1024)(128)(4,1)S(1)}, s32[]{:S(2)}) async-start(s8[8388608]{0:T(1024)(128)(4,1)} %bitcast.48), calls=%async_computation | async-start | bytes 8388608 | tf_op jit(solution)/shard_map/while
  104.3 24.0 %slice-start.1 = ((s8[8388608]{0:T(1024)(128)(4,1)}), s8[4194304]{0:T(1024)(128)(4,1)S(1)}, s32[]{:S(2)}) async-start(s8[8388608]{0:T(1024)(128)(4,1)} %bitcast.48), calls=%async_computation.1 | async-start | bytes 8388608 | tf_op jit(solution)/shard_map/while
  128.3 8.3 %slice-start.2 = ((s8[8388608]{0:T(1024)(128)(4,1)}), s8[4194304]{0:T(1024)(128)(4,1)S(1)}, s32[]{:S(2)}) async-start(s8[8388608]{0:T(1024)(128)(4,1)} %bitcast.50), calls=%async_computation.2 | async-start | bytes 8388608 | tf_op jit(solution)/shard_map/while
  128.3 8.2 %slice-start.3 = ((s8[8388608]{0:T(1024)(128)(4,1)}), s8[4194304]{0:T(1024)(128)(4,1)S(1)}, s32[]{:S(2)}) async-start(s8[8388608]{0:T(1024)(128)(4,1)} %bitcast.50), calls=%async_computation.3 | async-start | bytes 8388608 | tf_op jit(solution)/shard_map/while
  149.4 29.6 %copy-start.3 = (f32[4,128,128]{2,1,0:T(8,128)S(1)}, f32[4,128,128]{2,1,0:T(8,128)}, u32[]{:S(2)}) copy-start(f32[4,128,128]{2,1,0:T(8,128)} %get-tuple-element.285) | copy-start | bytes 786436 | tf_op jit(solution)/shard_map/while
  153.9 26.0 %collective-permute-start = (f32[1,2,16,1,128,128]{5,4,3,2,1,0:T(8,128)}, f32[1,2,16,1,128,128]{5,4,3,2,1,0:T(8,128)}, u32[]{:S(2)}, u32[]{:S(2)}) collective-permute-start(f32[1,2,16,1,128,128]{5,4,3,2,1,0:T(8,128)} %get-tuple-element.260), channel_id=1, source_target_pairs={{0,1},{1,2},{2,3},{3,4},{4,5},{5,6},{6,7},{8,9},{9,10},{10,11},{11... | collective-permute-start | bytes 6291464 | tf_op jit(solution)/shard_map/while/body/eval_jaxpr/ppermute | solution.py:23
  177.1 6.4 collective-permute-start.1
  183.4 24.0 %slice-start = ((s8[8388608]{0:T(1024)(128)(4,1)}), s8[4194304]{0:T(1024)(128)(4,1)S(1)}, s32[]{:S(2)}) async-start(s8[8388608]{0:T(1024)(128)(4,1)} %bitcast.48), calls=%async_computation | async-start | bytes 8388608 | tf_op jit(solution)/shard_map/while
  183.4 24.0 %slice-start.1 = ((s8[8388608]{0:T(1024)(128)(4,1)}), s8[4194304]{0:T(1024)(128)(4,1)S(1)}, s32[]{:S(2)}) async-start(s8[8388608]{0:T(1024)(128)(4,1)} %bitcast.48), calls=%async_computation.1 | async-start | bytes 8388608 | tf_op jit(solution)/shard_map/while
  207.4 8.3 %slice-start.2 = ((s8[8388608]{0:T(1024)(128)(4,1)}), s8[4194304]{0:T(1024)(128)(4,1)S(1)}, s32[]{:S(2)}) async-start(s8[8388608]{0:T(1024)(128)(4,1)} %bitcast.50), calls=%async_computation.2 | async-start | bytes 8388608 | tf_op jit(solution)/shard_map/while
  207.4 8.2 %slice-start.3 = ((s8[8388608]{0:T(1024)(128)(4,1)}), s8[4194304]{0:T(1024)(128)(4,1)S(1)}, s32[]{:S(2)}) async-start(s8[8388608]{0:T(1024)(128)(4,1)} %bitcast.50), calls=%async_computation.3 | async-start | bytes 8388608 | tf_op jit(solution)/shard_map/while
  228.5 29.6 %copy-start.3 = (f32[4,128,128]{2,1,0:T(8,128)S(1)}, f32[4,128,128]{2,1,0:T(8,128)}, u32[]{:S(2)}) copy-start(f32[4,128,128]{2,1,0:T(8,128)} %get-tuple-element.285) | copy-start | bytes 786436 | tf_op jit(solution)/shard_map/while
  233.0 26.0 %collective-permute-start = (f32[1,2,16,1,128,128]{5,4,3,2,1,0:T(8,128)}, f32[1,2,16,1,128,128]{5,4,3,2,1,0:T(8,128)}, u32[]{:S(2)}, u32[]{:S(2)}) collective-permute-start(f32[1,2,16,1,128,128]{5,4,3,2,1,0:T(8,128)} %get-tuple-element.260), channel_id=1, source_target_pairs={{0,1},{1,2},{2,3},{3,4},{4,5},{5,6},{6,7},{8,9},{9,10},{10,11},{11... | collective-permute-start | bytes 6291464 | tf_op jit(solution)/shard_map/while/body/eval_jaxpr/ppermute | solution.py:23
  256.2 6.4 collective-permute-start.1
  262.6 24.0 %slice-start = ((s8[8388608]{0:T(1024)(128)(4,1)}), s8[4194304]{0:T(1024)(128)(4,1)S(1)}, s32[]{:S(2)}) async-start(s8[8388608]{0:T(1024)(128)(4,1)} %bitcast.48), calls=%async_computation | async-start | bytes 8388608 | tf_op jit(solution)/shard_map/while
  262.6 24.0 %slice-start.1 = ((s8[8388608]{0:T(1024)(128)(4,1)}), s8[4194304]{0:T(1024)(128)(4,1)S(1)}, s32[]{:S(2)}) async-start(s8[8388608]{0:T(1024)(128)(4,1)} %bitcast.48), calls=%async_computation.1 | async-start | bytes 8388608 | tf_op jit(solution)/shard_map/while
  286.5 8.3 %slice-start.2 = ((s8[8388608]{0:T(1024)(128)(4,1)}), s8[4194304]{0:T(1024)(128)(4,1)S(1)}, s32[]{:S(2)}) async-start(s8[8388608]{0:T(1024)(128)(4,1)} %bitcast.50), calls=%async_computation.2 | async-start | bytes 8388608 | tf_op jit(solution)/shard_map/while
  286.6 8.2 %slice-start.3 = ((s8[8388608]{0:T(1024)(128)(4,1)}), s8[4194304]{0:T(1024)(128)(4,1)S(1)}, s32[]{:S(2)}) async-start(s8[8388608]{0:T(1024)(128)(4,1)} %bitcast.50), calls=%async_computation.3 | async-start | bytes 8388608 | tf_op jit(solution)/shard_map/while
  307.7 29.6 %copy-start.3 = (f32[4,128,128]{2,1,0:T(8,128)S(1)}, f32[4,128,128]{2,1,0:T(8,128)}, u32[]{:S(2)}) copy-start(f32[4,128,128]{2,1,0:T(8,128)} %get-tuple-element.285) | copy-start | bytes 786436 | tf_op jit(solution)/shard_map/while
  312.1 26.0 %collective-permute-start = (f32[1,2,16,1,128,128]{5,4,3,2,1,0:T(8,128)}, f32[1,2,16,1,128,128]{5,4,3,2,1,0:T(8,128)}, u32[]{:S(2)}, u32[]{:S(2)}) collective-permute-start(f32[1,2,16,1,128,128]{5,4,3,2,1,0:T(8,128)} %get-tuple-element.260), channel_id=1, source_target_pairs={{0,1},{1,2},{2,3},{3,4},{4,5},{5,6},{6,7},{8,9},{9,10},{10,11},{11... | collective-permute-start | bytes 6291464 | tf_op jit(solution)/shard_map/while/body/eval_jaxpr/ppermute | solution.py:23
  335.3 6.4 collective-permute-start.1
  341.7 24.0 %slice-start = ((s8[8388608]{0:T(1024)(128)(4,1)}), s8[4194304]{0:T(1024)(128)(4,1)S(1)}, s32[]{:S(2)}) async-start(s8[8388608]{0:T(1024)(128)(4,1)} %bitcast.48), calls=%async_computation | async-start | bytes 8388608 | tf_op jit(solution)/shard_map/while
  341.7 24.0 %slice-start.1 = ((s8[8388608]{0:T(1024)(128)(4,1)}), s8[4194304]{0:T(1024)(128)(4,1)S(1)}, s32[]{:S(2)}) async-start(s8[8388608]{0:T(1024)(128)(4,1)} %bitcast.48), calls=%async_computation.1 | async-start | bytes 8388608 | tf_op jit(solution)/shard_map/while
  365.7 8.3 %slice-start.2 = ((s8[8388608]{0:T(1024)(128)(4,1)}), s8[4194304]{0:T(1024)(128)(4,1)S(1)}, s32[]{:S(2)}) async-start(s8[8388608]{0:T(1024)(128)(4,1)} %bitcast.50), calls=%async_computation.2 | async-start | bytes 8388608 | tf_op jit(solution)/shard_map/while
  365.7 8.2 %slice-start.3 = ((s8[8388608]{0:T(1024)(128)(4,1)}), s8[4194304]{0:T(1024)(128)(4,1)S(1)}, s32[]{:S(2)}) async-start(s8[8388608]{0:T(1024)(128)(4,1)} %bitcast.50), calls=%async_computation.3 | async-start | bytes 8388608 | tf_op jit(solution)/shard_map/while
  386.8 29.6 %copy-start.3 = (f32[4,128,128]{2,1,0:T(8,128)S(1)}, f32[4,128,128]{2,1,0:T(8,128)}, u32[]{:S(2)}) copy-start(f32[4,128,128]{2,1,0:T(8,128)} %get-tuple-element.285) | copy-start | bytes 786436 | tf_op jit(solution)/shard_map/while
  391.3 26.0 %collective-permute-start = (f32[1,2,16,1,128,128]{5,4,3,2,1,0:T(8,128)}, f32[1,2,16,1,128,128]{5,4,3,2,1,0:T(8,128)}, u32[]{:S(2)}, u32[]{:S(2)}) collective-permute-start(f32[1,2,16,1,128,128]{5,4,3,2,1,0:T(8,128)} %get-tuple-element.260), channel_id=1, source_target_pairs={{0,1},{1,2},{2,3},{3,4},{4,5},{5,6},{6,7},{8,9},{9,10},{10,11},{11... | collective-permute-start | bytes 6291464 | tf_op jit(solution)/shard_map/while/body/eval_jaxpr/ppermute | solution.py:23
  414.5 6.4 collective-permute-start.1
  420.9 24.0 %slice-start = ((s8[8388608]{0:T(1024)(128)(4,1)}), s8[4194304]{0:T(1024)(128)(4,1)S(1)}, s32[]{:S(2)}) async-start(s8[8388608]{0:T(1024)(128)(4,1)} %bitcast.48), calls=%async_computation | async-start | bytes 8388608 | tf_op jit(solution)/shard_map/while
  420.9 24.0 %slice-start.1 = ((s8[8388608]{0:T(1024)(128)(4,1)}), s8[4194304]{0:T(1024)(128)(4,1)S(1)}, s32[]{:S(2)}) async-start(s8[8388608]{0:T(1024)(128)(4,1)} %bitcast.48), calls=%async_computation.1 | async-start | bytes 8388608 | tf_op jit(solution)/shard_map/while
  444.8 8.3 %slice-start.2 = ((s8[8388608]{0:T(1024)(128)(4,1)}), s8[4194304]{0:T(1024)(128)(4,1)S(1)}, s32[]{:S(2)}) async-start(s8[8388608]{0:T(1024)(128)(4,1)} %bitcast.50), calls=%async_computation.2 | async-start | bytes 8388608 | tf_op jit(solution)/shard_map/while
  444.9 8.2 %slice-start.3 = ((s8[8388608]{0:T(1024)(128)(4,1)}), s8[4194304]{0:T(1024)(128)(4,1)S(1)}, s32[]{:S(2)}) async-start(s8[8388608]{0:T(1024)(128)(4,1)} %bitcast.50), calls=%async_computation.3 | async-start | bytes 8388608 | tf_op jit(solution)/shard_map/while
  473.2 27.4 %copy-start.4 = (f32[4]{0:T(128)S(1)}, f32[4]{0:T(128)}, u32[]{:S(2)}) copy-start(f32[4]{0:T(128)} %param.13) | copy-start | bytes 52
  473.2 28.8 %copy-start.2 = (f32[2,16,65536]{2,1,0:T(8,128)S(1)}, f32[2,16,65536]{2,1,0:T(8,128)}, u32[]{:S(2)}) copy-start(f32[2,16,65536]{2,1,0:T(8,128)} %reshape.188) | copy-start | bytes 25165828
  563.3 88.9 %collective-permute-start.2 = (f32[16,65536]{1,0:T(8,128)S(1)}, f32[16,65536]{1,0:T(8,128)S(1)}, u32[]{:S(2)}, u32[]{:S(2)}) collective-permute-start(f32[16,65536]{1,0:T(8,128)S(1)} %convolution_bitcast_fusion), channel_id=1, source_target_pairs={{0,8},{8,0},{16,24},{24,16},{1,9},{9,1},{17,25},{25,17},{2,10},{10... | collective-permute-start | bytes 12582920 | tf_op jit(solution)/shard_map/ppermute | solution.py:14
  652.7 88.1 %collective-permute-start.3 = (f32[16,65536]{1,0:T(8,128)S(1)}, f32[16,65536]{1,0:T(8,128)S(1)}, u32[]{:S(2)}, u32[]{:S(2)}) collective-permute-start(f32[16,65536]{1,0:T(8,128)S(1)} %add.186), channel_id=1, source_target_pairs={{0,16},{8,24},{16,0},{24,8},{1,17},{9,25},{17,1},{25,9},{2,18},{10... | collective-permute-start | bytes 12582920 | tf_op jit(solution)/shard_map/ppermute | solution.py:14
  (10 other events, 37.3 us)
